TPU v7x, 32 devices: a whole 2x2x4 slice. The times are simulated.
32 devices in a mesh: dp: 4 (over y, x), mp: 8 (over z, core).
Axes of the slice: x: 2, y: 2, z: 4, core: 2. Of those that a mesh axis runs over, the one named last changes fastest.
Arguments:
- rewards: int32 [32], P('dp'), may hold values from 0 to 4096, as said below
- group_ids: int32 [32], P('dp'), may hold values from 0 to 1, as said below
- lengths: int32 [32], P('dp'), may hold values from 1 to 64
- token_mask: int32 [2048], P('dp'), may hold values from 0 to 1, as said below
- targets: int32 [2048], P('dp'), may hold values from 0 to 65535
- logits: bfloat16 [2048, 65536], P('dp', 'mp'), may hold values from -140 to 400
Outputs:
- advantage: float32 [32], P('dp')
- token_weight: float32 [2048], P('dp')
- token_logprob: float32 [2048], P('dp')
- token_entropy: float32 [2048], P('dp')
- objective: float32 [], replicated
Inputs may be any that keep to these rules, and one draw needn't show every extreme that they name: rewards in units of 1/1024. `group_ids`: each of the 2 prompts has exactly 16 trajectories. `token_mask`: zeros come in aligned spans of 8 positions, except that the first position of each window is always 1.
All inputs are finite; a program needn't handle non-finite values.
Results may differ from a plain program's by a relative error of at most 0.00095.
Values may be sent and summed in bfloat16 or wider, within the bound.
A program may use at most 64 MiB of HBM per device.

v0:
```python
import jax
import jax.numpy as jnp
from jax import lax
from jax.sharding import PartitionSpec as P

GROUP = 16
WIN = 64


spread_floor = 0.25
reward_unit = 1024.0
highest = lax.Precision.HIGHEST


def table_dot(left_side, right_side):
    return jnp.dot(left_side, right_side, precision=highest)


def quarter_rows(source, rollouts, quarter, slot_index):
    shaped = source.reshape((rollouts, 4, quarter) + source.shape[1:])
    return shaped[:, slot_index].reshape((rollouts * quarter,) + source.shape[1:])


def join_quarters(pieces, rollouts, quarter):
    stacked = jnp.stack([portion.reshape(rollouts, quarter) for portion in pieces], axis=1)
    return stacked.reshape(rollouts * 4 * quarter)


def tile_peak(logit_tile):
    return jnp.max(logit_tile, axis=1).astype(jnp.float32)


def zero_peak(logit_tile):
    return jnp.zeros((logit_tile.shape[0],), jnp.float32)


def shifted_sums(logit_tile, row_shift):
    shifted = logit_tile.astype(jnp.float32) - row_shift[:, None]
    weights = jnp.exp(shifted)
    return (jnp.sum(weights, axis=1), jnp.sum(weights * shifted, axis=1))


def empty_sums(logit_tile, row_shift):
    height = logit_tile.shape[0]
    return (jnp.ones((height,), jnp.float32), jnp.zeros((height,), jnp.float32))


def own_stats(logit_tile):
    row_peak = tile_peak(logit_tile)
    totals, moments = shifted_sums(logit_tile, row_peak)
    return (row_peak, totals, moments)


def empty_stats(logit_tile):
    height = logit_tile.shape[0]
    return (
        jnp.zeros((height,), jnp.float32),
        jnp.ones((height,), jnp.float32),
        jnp.zeros((height,), jnp.float32),
    )


def shards(rewards, group_ids, lengths, token_mask, targets, logits):
    rollouts = lengths.shape[0]
    vocab_dev = logits.shape[1]
    quarter = WIN // 4
    positions = jnp.arange(WIN, dtype=jnp.int32)
    live_mask = (
        (token_mask.reshape(rollouts, WIN) > 0) & (positions[None, :] < lengths[:, None])
    ).astype(jnp.float32)
    longest = jnp.max(lengths)
    local_index = targets - lax.axis_index("mp") * vocab_dev
    inside = (local_index >= 0) & (local_index < vocab_dev)
    picked = jnp.take_along_axis(logits, jnp.clip(local_index, 0, vocab_dev - 1)[:, None], axis=1)[
        :, 0
    ]
    target_share = jnp.where(inside, picked.astype(jnp.float32), 0.0)
    logit_tiles = [quarter_rows(logits, rollouts, quarter, slot_index) for slot_index in range(4)]
    last_tile = logit_tiles[3]
    last_stats = lax.cond(longest <= 3 * quarter, empty_stats, own_stats, last_tile)
    tile_peaks = [
        lax.cond(longest > slot_index * quarter, tile_peak, zero_peak, logit_tiles[slot_index])
        for slot_index in range(3)
    ]
    tile_peaks.append(last_stats[0])
    row_peak = lax.pmax(join_quarters(tile_peaks, rollouts, quarter), "mp")
    peak_tiles = [quarter_rows(row_peak, rollouts, quarter, slot_index) for slot_index in range(4)]
    sum_tiles = []
    moment_tiles = []
    for slot_index in range(3):
        tile_sums = lax.cond(
            longest > slot_index * quarter,
            shifted_sums,
            empty_sums,
            logit_tiles[slot_index],
            peak_tiles[slot_index],
        )
        sum_tiles.append(tile_sums[0])
        moment_tiles.append(tile_sums[1])
    last_peak, last_total, last_moment = last_stats
    peak_gap = last_peak - peak_tiles[3]
    factor = jnp.exp(peak_gap)
    sum_tiles.append(factor * last_total)
    moment_tiles.append(factor * (last_moment + peak_gap * last_total))
    row_total, row_moment, target_logit = lax.psum(
        (
            join_quarters(sum_tiles, rollouts, quarter),
            join_quarters(moment_tiles, rollouts, quarter),
            target_share,
        ),
        "mp",
    )
    log_total = row_peak + jnp.log(row_total)
    log_prob = target_logit - log_total
    entropy = jnp.log(row_total) - row_moment / row_total
    token_logprob = live_mask * log_prob.reshape(rollouts, WIN)
    token_entropy = live_mask * entropy.reshape(rollouts, WIN)
    counts = jnp.sum(live_mask, axis=1)
    reward_values = rewards.astype(jnp.float32) / reward_unit
    groups = rollouts * lax.axis_size("dp") // GROUP
    member = (group_ids[:, None] == jnp.arange(groups, dtype=jnp.int32)[None, :]).astype(
        jnp.float32
    )
    rollout_sums = jnp.sum(token_logprob, axis=1)
    sum_reward, sum_square, group_tokens, sum_product, sum_logprob = lax.psum(
        (
            table_dot(reward_values, member),
            table_dot(reward_values * reward_values, member),
            table_dot(counts, member),
            table_dot(reward_values * rollout_sums, member),
            table_dot(rollout_sums, member),
        ),
        "dp",
    )
    group_mean = sum_reward / GROUP
    group_var = jnp.maximum(sum_square / GROUP - group_mean * group_mean, 0.0)
    group_spread = jnp.maximum(jnp.sqrt(group_var), spread_floor)
    centred = reward_values - table_dot(member, group_mean)
    advantage = centred / table_dot(member, group_spread)
    token_scale = GROUP * WIN / table_dot(member, group_tokens)
    token_weight = live_mask * (advantage * token_scale)[:, None]
    total_rows = groups * GROUP * WIN
    group_terms = (
        GROUP * WIN / group_tokens * (sum_product - group_mean * sum_logprob) / group_spread
    )
    objective = -jnp.sum(group_terms) / total_rows
    return (
        advantage,
        token_weight.reshape(-1),
        token_logprob.reshape(-1),
        token_entropy.reshape(-1),
        objective,
    )


def solution(mesh):
    in_specs = (P("dp"), P("dp"), P("dp"), P("dp"), P("dp"), P("dp", "mp"))
    out_specs = (P("dp"), P("dp"), P("dp"), P("dp"), P())
    return jax.shard_map(shards, mesh=mesh, in_specs=in_specs, out_specs=out_specs, check_vma=False)
```

profile of v0, /device:TPU:0, one launch (start us, length us, event | category | flops | bytes accessed | tf_op | source)
XLA Modules:
  0.0 88.0 jit_solution(6986217275774136126)
XLA Ops:
  0.6 1.3 %reduce_max.45 = s32[]{:T(128)} reduce(s32[8]{0:T(128)} %param.22, s32[]{:T(128)} %constant.67.clone.1), dimensions={0}, to_apply=%region_5.6 | reduce | flops 7 | bytes 40 | tf_op jit(solution)/shard_map/reduce_max | solution.py:71
  4.5 0.9 convolution_bitcast_fusion.5
  5.4 0.9 convolution_bitcast_fusion.7
  6.2 0.7 iota_compare_fusion
  7.0 0.1 lt.35
  7.1 0.7 compare_select_fusion
  7.8 8.1 %gather_fusion = bf16[512]{0:T(512)(128)(2,1)S(1)} fusion(bf16[512,8192]{1,0:T(8,128)(2,1)} %param.25, s32[512]{0:T(512)S(1)} %bitcast.64), kind=kCustom, calls=%fused_computation | custom fusion | bytes 6144 | tf_op jit(solution)/shard_map/jit(take_along_axis)/gather | solution.py:74
  15.9 0.7 convert_select_fusion
  16.6 5.4 %fusion.28 = (bf16[8,1,16,8192]{3,2,1,0:T(8,128)(2,1)S(1)}, bf16[8,1,16,8192]{3,2,1,0:T(8,128)(2,1)}, bf16[8,1,16,8192]{3,2,1,0:T(8,128)(2,1)}) fusion(bf16[8,4,16,8192]{3,2,1,0:T(8,128)(2,1)} %bitcast.72), kind=kLoop, calls=%fused_computation.78 | loop fusion | bytes 12582912 | tf_op jit(solution)/shard_map/slice | solution.py:21
  22.0 0.4 conditional.7
  22.0 0.4 reduce_max.40
  22.4 0.1 reshape.148
  22.5 2.1 %conditional.8 = (f32[8,1,16]{2,0,1:T(8,128)S(1)}) conditional(s32[]{:T(128)} %convert_element_type.99, () %tuple.79, bf16[128,8192]{1,0:T(8,128)(2,1)} %bitcast.67), branch_computations={%region_9.10_spmd, %region_10.12_spmd} | conditional | flops 1048448 | bytes 2098186 | solution.py:82
  22.5 2.0 %reduce_max.41 = bf16[128]{0:T(256)(128)(2,1)S(1)} reduce(bf16[128,8192]{1,0:T(8,128)(2,1)} %param.3, bf16[]{:T(256)} %constant.19.clone), dimensions={1}, to_apply=%region_11.11 | reduce | flops 1048448 | bytes 2097410 | tf_op jit(solution)/shard_map/cond/branch_1_fun/reduce_max | solution.py:30
  24.5 0.1 reshape.149
  24.6 0.1 reshape.143
  24.7 18.0 %pmax.7 = f32[512]{0:T(512)S(1)} all-reduce(f32[512]{0:T(512)S(1)} %reshape.143), channel_id=1, replica_groups=mesh['dp'=4,'mp'=8] {'mp'}, use_global_device_ids=true, to_apply=%region_20.21 | all-reduce | flops 512 | bytes 4096 | tf_op jit(solution)/shard_map/pmax | solution.py:86
  42.7 0.1 reshape.144
  42.8 3.1 %conditional.12 = (f32[8,1,16]{2,0,1:T(8,128)S(1)}, f32[8,1,16]{2,0,1:T(8,128)S(1)}) conditional(s32[]{:T(128)} %convert_element_type.99, () %tuple.84, (bf16[128,8192]{1,0:T(8,128)(2,1)}, f32[8,4,16]{2,1,0:T(4,128)S(1)}) %tuple.122), branch_computations={%region_25.26_spmd, %region_26.29_spmd} | conditional | flops 5242624 | bytes 2106896 | solution.py:91
  42.8 0.1 sub.50
  42.9 2.8 %fusion.2 = (f32[128]{0:T(128)S(1)}, f32[128]{0:T(128)S(1)}) fusion(bf16[128,8192]{1,0:T(8,128)(2,1)} %get-tuple-element.42, f32[128]{0:T(128)S(1)} %sub.50), kind=kLoop, calls=%fused_computation.13 | loop fusion | flops 5242624 | bytes 2098688 | tf_op jit(solution)/shard_map/cond/branch_1_fun/reduce_sum | solution.py:40
  45.8 0.1 stack_reshape.61
  45.8 0.1 stack_reshape.60
  45.9 1.5 %conditional.11 = (f32[8,1,16]{2,0,1:T(8,128)S(1)}, f32[8,1,16]{2,0,1:T(8,128)S(1)}) conditional(s32[]{:T(128)} %convert_element_type.98, () %tuple.82, (bf16[128,8192]{1,0:T(8,128)(2,1)S(1)}, f32[8,4,16]{2,1,0:T(4,128)S(1)}) %tuple.121), branch_computations={%region_21.22_spmd, %region_22.25_spmd} | conditional | flops 5242624 | bytes 2106896 | solution.py:91
  45.9 0.1 sub.39
  46.0 1.3 %fusion.1 = (f32[128]{0:T(128)S(1)}, f32[128]{0:T(128)S(1)}) fusion(bf16[128,8192]{1,0:T(8,128)(2,1)S(1)} %get-tuple-element.40, f32[128]{0:T(128)S(1)} %sub.39), kind=kLoop, calls=%fused_computation.9 | loop fusion | flops 5242624 | bytes 2098688 | tf_op jit(solution)/shard_map/cond/branch_1_fun/reduce_sum | solution.py:40
  47.3 0.1 stack_reshape.57
  47.4 0.1 stack_reshape.56
  47.5 0.1 reshape_squeeze.28
  47.6 0.1 stack_reshape.69
  47.6 0.1 stack_reshape.68
  47.7 0.1 reshape.145
  47.8 0.1 reshape.146
  47.9 13.9 %all-reduce = (f32[512]{0:T(512)S(1)}, f32[512]{0:T(512)S(1)}, f32[512]{0:T(512)S(1)}) all-reduce(f32[512]{0:T(512)S(1)} %convert_select_fusion, f32[512]{0:T(512)S(1)} %reshape.145, f32[512]{0:T(512)S(1)} %reshape.146), channel_id=1, replica_groups=mesh['dp'=4,'mp'=8] {'mp'}, use_global_device_ids=true, to_apply=%region_4.5 | all-reduce | flops 1536 | bytes 12288 | tf_op jit(solution)/shard_map/psum | solution.py:105
  61.8 0.6 subtract_select_fusion
  62.4 0.6 broadcast_select_fusion
  63.0 0.1 gt.26
  63.2 0.2 select_reduce_fusion
  63.4 0.2 convolution_bitcast_fusion.3
  63.5 0.2 convolution_bitcast_fusion
  63.7 0.2 convolution_bitcast_fusion.1
  63.9 20.3 %all-reduce.1 = (f32[2]{0:T(128)S(1)}, f32[2]{0:T(128)S(1)}, f32[2]{0:T(128)S(1)}, f32[2]{0:T(128)S(1)}, f32[2]{0:T(128)S(1)}) all-reduce(f32[2]{0:T(128)S(1)} %convolution_bitcast_fusion.5, f32[2]{0:T(128)S(1)} %convolution_bitcast_fusion.7, f32[2]{0:T(128)S(1)} %convolution_bitcast_fusion.3, ...), channel_id=1, replica_groups=mesh['dp'=4,'mp'=8] {'dp'}, use_global_device_ids=true, to_apply=%region_1.2 | all-reduce | flops 10 | bytes 80 | tf_op jit(solution)/shard_map/psum | solution.py:125
  84.2 0.6 fusion.26
  85.5 0.2 convolution_bitcast_fusion.4
  85.7 0.2 fusion.5
  85.9 0.2 fusion.7
  86.2 0.1 mul.65
  86.2 0.6 broadcast_select_fusion.1
  (36 shorter events, 0.4 us)
Async XLA Ops:
  22.5 39.4 %copy-start = (s32[512]{0:T(512)S(1)}, s32[512]{0:T(512)}, u32[]{:S(2)}) copy-start(s32[512]{0:T(512)} %param.23) | copy-start | bytes 6148
  22.5 40.7 %copy-start.1 = (s32[8]{0:T(128)S(1)}, s32[8]{0:T(128)}, u32[]{:S(2)}) copy-start(s32[8]{0:T(128)} %param.22) | copy-start | bytes 100
  22.5 40.9 %copy-start.3 = (s32[8]{0:T(128)S(1)}, s32[8]{0:T(128)}, u32[]{:S(2)}) copy-start(s32[8]{0:T(128)} %param.21) | copy-start | bytes 100
  22.5 41.2 %copy-start.2 = (s32[8]{0:T(128)S(1)}, s32[8]{0:T(128)}, u32[]{:S(2)}) copy-start(s32[8]{0:T(128)} %param.20) | copy-start | bytes 100
  85.9 1.0 %copy-start.4 = (f32[8]{0:T(128)}, f32[8]{0:T(128)S(1)}, u32[]{:S(2)}) copy-start(f32[8]{0:T(128)S(1)} %fusion.5) | copy-start | bytes 100
where the time goes:
time: 88.5 us; the launch traced here: 88 us
  blocking collectives  52.2 us (59%)
  local copies, waits for them, and re-layouts  15.2 us (17%)
  other arithmetic  12.5 us (14%)
  between operations  5.13 us (6%)
  matrix products  2.85 us (3%)
    psum x1, blocking collectives, shards(): lax.psum((table_dot(reward_values, member), table_dot(reward_values * rew...  20.3 us
    pmax x1, blocking collectives, shards(): row_peak = lax.pmax(join_quarters(tile_peaks, rollouts, quarter), 'mp')  18 us
    psum x1, blocking collectives, shards(): lax.psum((join_quarters(sum_tiles, rollouts, quarter), join_quarters(mome...  13.9 us
    gather x1, local copies, waits for them, and re-layouts, shards(): jnp.take_along_axis(logits, jnp.clip(local_index, 0, vocab_dev - 1)[:, No...  8.1 us
    slice x4, local copies, waits for them, and re-layouts, quarter_rows(): shaped[:, slot_index].reshape((rollouts * quarter,) + source.shape[1:])  5.44 us
    reduce_sum x2, other arithmetic, shifted_sums(): return (jnp.sum(weights, axis=1), jnp.sum(weights * shifted, axis=1))  4.11 us
    dot_general x8, matrix products, table_dot(): return jnp.dot(left_side, right_side, precision=highest)  2.85 us
    reduce_max x2, other arithmetic, tile_peak(): return jnp.max(logit_tile, axis=1).astype(jnp.float32)  2.32 us

commit v1 on v0

v1 whole, which is shorter than its diff:
```python
import functools

import jax
import jax.numpy as jnp
from jax import lax
from jax.experimental import pallas as pl
from jax.experimental.pallas import tpu as pltpu
from jax.sharding import PartitionSpec as P

GROUP = 16
WIN = 64
LANES = 128
STEP = 16
CHUNKS = 8

spread_floor = 0.25
reward_unit = 1024.0
MESH = pl.DeviceIdType.MESH


def each(first, last, visit):
    if last - first <= 16:
        for k in range(first, last):
            visit(k)
    else:
        lax.fori_loop(first, last, lambda k, carry: (visit(k), carry)[1], 0)


def kernel(
    dp_size,
    mp_size,
    rewards_s,
    groups_s,
    lengths_s,
    rewards_v,
    groups_v,
    mask_v,
    targets_v,
    logits_hbm,
    advantage_out,
    weight_out,
    logprob_out,
    entropy_out,
    objective_out,
    *scratch,
):
    chunks = scratch[:CHUNKS]
    (
        peak_rows,
        total_rows_ref,
        moment_rows,
        target_rows,
        columns,
        stats,
        gathered,
        facts,
        facts_all,
        part,
        parts,
        load_sem,
        stat_send,
        stat_recv,
        fact_send,
        fact_recv,
        part_send,
        part_recv,
    ) = scratch[CHUNKS:]
    rows, vocab = logits_hbm.shape
    rollouts = rewards_v.shape[1]
    bands = rows // LANES
    groups = rollouts * dp_size // GROUP
    chunk_rows = rows // CHUNKS
    tiles = vocab // LANES
    me_dp = lax.axis_index("dp")
    me_mp = lax.axis_index("mp")
    f32 = jnp.float32

    loads = [
        pltpu.make_async_copy(
            logits_hbm.at[pl.ds(c * chunk_rows, chunk_rows), :], chunks[c], load_sem.at[c]
        )
        for c in range(CHUNKS)
    ]
    for load in loads:
        load.start()

    barrier = pltpu.get_barrier_semaphore()

    def greet_mp(k):
        peer = lax.rem(me_mp + k, mp_size)
        pl.semaphore_signal(barrier, inc=1, device_id=(me_dp, peer), device_id_type=MESH)

    def greet_dp(k):
        peer = lax.rem(me_dp + k, dp_size)
        pl.semaphore_signal(barrier, inc=1, device_id=(peer, me_mp), device_id_type=MESH)

    each(1, mp_size, greet_mp)
    each(1, dp_size, greet_dp)

    lane = lax.broadcasted_iota(jnp.int32, (bands, LANES), 1)
    band = lax.broadcasted_iota(jnp.int32, (bands, LANES), 0)
    owner = band * (LANES // WIN) + lane // WIN
    position = lax.rem(lane, WIN)
    reward_tok = jnp.zeros((bands, LANES), jnp.int32)
    group_tok = jnp.zeros((bands, LANES), jnp.int32)
    length_tok = jnp.zeros((bands, LANES), jnp.int32)
    for k in range(rollouts):
        here = owner == k
        reward_tok = jnp.where(here, rewards_s[k], reward_tok)
        group_tok = jnp.where(here, groups_s[k], group_tok)
        length_tok = jnp.where(here, lengths_s[k], length_tok)
    live = jnp.where((mask_v[...] > 0) & (position < length_tok), 1.0, 0.0).astype(f32)
    reward_tok = reward_tok.astype(f32) / reward_unit
    facts[0:bands, :] = reward_tok
    facts[bands : 2 * bands, :] = group_tok.astype(f32)
    facts[2 * bands : 3 * bands, :] = live

    base = me_mp * vocab
    for b in range(bands):
        spread_out = jnp.broadcast_to(targets_v[b : b + 1, :], (LANES, LANES))
        columns[b * LANES : (b + 1) * LANES, :] = spread_out.T

    for c in range(CHUNKS):
        loads[c].wait()
        chunk = chunks[c]

        def step(i, carry, c=c, chunk=chunk):
            start = pl.multiple_of(i * STEP, STEP)
            where_out = pl.ds(pl.multiple_of(c * chunk_rows + i * STEP, STEP), STEP)
            span = pl.ds(start, STEP)
            column = lax.shift_right_arithmetic(columns[where_out, :] - base, 7)
            bits = [
                jnp.bitwise_and(lax.shift_right_arithmetic(column, k), 1).astype(f32)
                for k in range(max(tiles - 1, 0).bit_length())
            ]
            bits = [bit.astype(jnp.bfloat16) > 0.5 for bit in bits]

            def survey(first, size):
                if size == 1:
                    tile = chunk[span, first * LANES : (first + 1) * LANES]
                    return tile, tile
                half = size // 2
                low = survey(first, half)
                if first + half >= tiles:
                    return low
                top = survey(first + half, half)
                chosen = jnp.where(bits[half.bit_length() - 1], top[1], low[1])
                return jnp.maximum(low[0], top[0]), chosen

            high, held = survey(0, 1 << max(tiles - 1, 0).bit_length())
            target_rows[where_out, :] = held.astype(f32)
            high = high.astype(f32)
            total = jnp.zeros((STEP, LANES), f32)
            moment = jnp.zeros((STEP, LANES), f32)
            for j in range(tiles):
                shifted = chunk[span, j * LANES : (j + 1) * LANES].astype(f32) - high
                weight = jnp.exp(shifted)
                total += weight
                moment += weight * shifted
            peak_rows[where_out, :] = high
            total_rows_ref[where_out, :] = total
            moment_rows[where_out, :] = moment
            return carry

        lax.fori_loop(0, chunk_rows // STEP, step, 0)

        if c == 0:
            pl.semaphore_wait(barrier, mp_size + dp_size - 2)

            def send_fact(k):
                peer = lax.rem(me_dp + k, dp_size)
                pltpu.make_async_remote_copy(
                    src_ref=facts,
                    dst_ref=facts_all.at[me_dp],
                    send_sem=fact_send.at[k],
                    recv_sem=fact_recv.at[me_dp],
                    device_id=(peer, me_mp),
                    device_id_type=MESH,
                ).start()

            each(1, dp_size, send_fact)

    sub = lax.broadcasted_iota(jnp.int32, (LANES, LANES), 0)
    for b in range(bands):
        block = slice(b * LANES, (b + 1) * LANES)
        high = peak_rows[block, :].T
        total = total_rows_ref[block, :].T
        moment = moment_rows[block, :].T
        held = target_rows[block, :].T
        peak = jnp.max(high, axis=0, keepdims=True)
        gap = high - peak
        factor = jnp.exp(gap)
        local = targets_v[b : b + 1, :] - base
        inside = (local >= 0) & (local < vocab)
        at_lane = jnp.where(inside, jnp.bitwise_and(local, LANES - 1), -1)
        stats[b : b + 1, :] = peak
        stats[bands + b : bands + b + 1, :] = jnp.sum(factor * total, axis=0, keepdims=True)
        stats[2 * bands + b : 2 * bands + b + 1, :] = jnp.sum(
            factor * (moment + gap * total), axis=0, keepdims=True
        )
        stats[3 * bands + b : 3 * bands + b + 1, :] = jnp.sum(
            jnp.where(sub == at_lane, held, 0.0), axis=0, keepdims=True
        )

    def stat_copy(k, slot):
        peer = lax.rem(me_mp + k, mp_size)
        return pltpu.make_async_remote_copy(
            src_ref=stats,
            dst_ref=gathered.at[slot],
            send_sem=stat_send.at[k],
            recv_sem=stat_recv.at[slot],
            device_id=(me_dp, peer),
            device_id_type=MESH,
        )

    each(1, mp_size, lambda k: stat_copy(k, me_mp).start())
    gathered[me_mp] = stats[...]

    def fact_copy(k, slot):
        peer = lax.rem(me_dp + k, dp_size)
        return pltpu.make_async_remote_copy(
            src_ref=facts,
            dst_ref=facts_all.at[slot],
            send_sem=fact_send.at[k],
            recv_sem=fact_recv.at[slot],
            device_id=(peer, me_mp),
            device_id_type=MESH,
        )

    facts_all[me_dp] = facts[...]
    each(1, dp_size, lambda k: fact_copy(k, lax.rem(me_dp + dp_size - k, dp_size)).wait_recv())
    all_reward = facts_all[:, 0:bands, :]
    all_group = facts_all[:, bands : 2 * bands, :]
    all_live = facts_all[:, 2 * bands : 3 * bands, :]

    def whole_sum(values):
        flat = jnp.sum(values, axis=0)
        return jnp.sum(jnp.sum(flat, axis=1, keepdims=True), axis=0, keepdims=True)

    reward_row = rewards_v[...].astype(f32) / reward_unit
    mean_row = jnp.zeros((1, rollouts), f32)
    spread_row = jnp.ones((1, rollouts), f32)
    mean_tok = jnp.zeros((bands, LANES), f32)
    spread_tok = jnp.ones((bands, LANES), f32)
    scale_tok = jnp.zeros((bands, LANES), f32)
    for g in range(groups):
        member = jnp.where(all_group == float(g), 1.0, 0.0).astype(f32)
        mean = whole_sum(member * all_reward) / (GROUP * WIN)
        apart = all_reward - mean[None]
        variance = whole_sum(member * apart * apart) / (GROUP * WIN)
        spread = jnp.maximum(jnp.sqrt(variance), spread_floor)
        scale = (GROUP * WIN) / whole_sum(member * all_live)
        in_row = groups_v[...] == g
        in_tok = group_tok == g
        mean_row = jnp.where(in_row, mean, mean_row)
        spread_row = jnp.where(in_row, spread, spread_row)
        mean_tok = jnp.where(in_tok, mean, mean_tok)
        spread_tok = jnp.where(in_tok, spread, spread_tok)
        scale_tok = jnp.where(in_tok, scale, scale_tok)
    advantage_out[...] = (reward_row - mean_row) / spread_row
    weight = live * ((reward_tok - mean_tok) / spread_tok * scale_tok)
    weight_out[...] = weight

    each(1, mp_size, lambda k: stat_copy(k, lax.rem(me_mp + mp_size - k, mp_size)).wait_recv())
    peaks = gathered[:, 0:bands, :]
    peak = jnp.max(peaks, axis=0)
    gap = peaks - peak[None]
    factor = jnp.exp(gap)
    totals = gathered[:, bands : 2 * bands, :]
    total = jnp.sum(factor * totals, axis=0)
    moment = jnp.sum(factor * (gathered[:, 2 * bands : 3 * bands, :] + gap * totals), axis=0)
    target = jnp.sum(gathered[:, 3 * bands : 4 * bands, :], axis=0)
    log_total = jnp.log(total)
    logprob = live * (target - (peak + log_total))
    logprob_out[...] = logprob
    own = jnp.sum(jnp.sum(weight * logprob, axis=1, keepdims=True), axis=0, keepdims=True)
    part[...] = jnp.broadcast_to(own, part.shape)

    def part_copy(k, slot):
        peer = lax.rem(me_dp + k, dp_size)
        return pltpu.make_async_remote_copy(
            src_ref=part,
            dst_ref=parts.at[slot],
            send_sem=part_send.at[k],
            recv_sem=part_recv.at[slot],
            device_id=(peer, me_mp),
            device_id_type=MESH,
        )

    each(1, dp_size, lambda k: part_copy(k, me_dp).start())
    parts[me_dp] = part[...]
    entropy_out[...] = live * (log_total - moment / total)

    each(1, dp_size, lambda k: fact_copy(k, me_dp).wait_send())
    each(1, mp_size, lambda k: stat_copy(k, me_mp).wait_send())
    each(1, dp_size, lambda k: part_copy(k, lax.rem(me_dp + dp_size - k, dp_size)).wait_recv())
    summed = jnp.sum(parts[...], axis=0)[0:1, 0:1]
    objective_out[...] = -summed / (groups * GROUP * WIN)
    each(1, dp_size, lambda k: part_copy(k, me_dp).wait_send())


def hand_over(*refs):
    half = len(refs) // 2
    for source, result in zip(refs[:half], refs[half:]):
        result[...] = source[...]


def shards(dp_size, mp_size, rewards, group_ids, lengths, token_mask, targets, logits):
    rows, vocab = logits.shape
    rollouts = lengths.shape[0]
    bands = rows // LANES
    f32 = jnp.float32
    smem = pl.BlockSpec(memory_space=pltpu.SMEM)
    vmem = pl.BlockSpec(memory_space=pltpu.VMEM)
    outs = pl.pallas_call(
        functools.partial(kernel, dp_size, mp_size),
        out_shape=(
            jax.ShapeDtypeStruct((1, rollouts), f32),
            jax.ShapeDtypeStruct((bands, LANES), f32),
            jax.ShapeDtypeStruct((bands, LANES), f32),
            jax.ShapeDtypeStruct((bands, LANES), f32),
            jax.ShapeDtypeStruct((1, 1), f32),
        ),
        in_specs=[smem] * 3 + [vmem] * 4 + [pl.BlockSpec(memory_space=pl.ANY)],
        out_specs=(vmem,) * 5,
        scratch_shapes=[pltpu.VMEM((rows // CHUNKS, vocab), logits.dtype)] * CHUNKS
        + [pltpu.VMEM((rows, LANES), f32)] * 4
        + [pltpu.VMEM((rows, LANES), jnp.int32)]
        + [
            pltpu.VMEM((4 * bands, LANES), f32),
            pltpu.VMEM((mp_size, 4 * bands, LANES), f32),
            pltpu.VMEM((3 * bands, LANES), f32),
            pltpu.VMEM((dp_size, 3 * bands, LANES), f32),
            pltpu.VMEM((8, LANES), f32),
            pltpu.VMEM((dp_size, 8, LANES), f32),
            pltpu.SemaphoreType.DMA((CHUNKS,)),
            pltpu.SemaphoreType.DMA((mp_size,)),
            pltpu.SemaphoreType.DMA((mp_size,)),
            pltpu.SemaphoreType.DMA((dp_size,)),
            pltpu.SemaphoreType.DMA((dp_size,)),
            pltpu.SemaphoreType.DMA((dp_size,)),
            pltpu.SemaphoreType.DMA((dp_size,)),
        ],
        compiler_params=pltpu.CompilerParams(collective_id=0, has_side_effects=True),
    )(
        rewards,
        group_ids,
        lengths,
        rewards.reshape(1, rollouts),
        group_ids.reshape(1, rollouts),
        token_mask.reshape(bands, LANES),
        targets.reshape(bands, LANES),
        logits,
    )
    outs = pl.pallas_call(
        hand_over,
        out_shape=[jax.ShapeDtypeStruct(value.shape, value.dtype) for value in outs],
        in_specs=[vmem] * 5,
        out_specs=[vmem] * 5,
    )(*outs)
    advantage, weight, logprob, entropy, objective = outs
    return (
        advantage.reshape(-1),
        weight.reshape(-1),
        logprob.reshape(-1),
        entropy.reshape(-1),
        objective.reshape(()),
    )


def solution(mesh):
    in_specs = (P("dp"), P("dp"), P("dp"), P("dp"), P("dp"), P("dp", "mp"))
    out_specs = (P("dp"), P("dp"), P("dp"), P("dp"), P())
    body = functools.partial(shards, mesh.shape["dp"], mesh.shape["mp"])
    return jax.shard_map(body, mesh=mesh, in_specs=in_specs, out_specs=out_specs, check_vma=False)
```

time: 88.5 us -> 23.3 us (0.26)
  blocking collectives: 52.2 us -> 0 us
  Pallas kernels: 0 us -> 22.5 us
  local copies, waits for them, and re-layouts: 15.2 us -> 0 us
  other arithmetic: 12.5 us -> 0 us
  between operations: 5.13 us -> 0.64 us
  matrix products: 2.85 us -> 0 us
    psum x2 -> x0, blocking collectives: 34.2 us -> none  [the longest x1 20.3 us: shards(): lax.psum((table_dot(reward_values, member), table_dot(reward_values * rew...]
    pallas_call x0 -> x2, Pallas kernels: none -> 22.5 us  [the longest x1 20.6 us: shards(): pl.pallas_call(functools.partial(kernel, dp_size, mp_size), out_shape=(ja...]
    pmax x1 -> x0, blocking collectives: 18 us -> none  [shards(): row_peak = lax.pmax(join_quarters(tile_peaks, rollouts, quarter), 'mp')]
    gather x1 -> x0, local copies, waits for them, and re-layouts: 8.1 us -> none  [shards(): jnp.take_along_axis(logits, jnp.clip(local_index, 0, vocab_dev - 1)[:, No...]
    slice x4 -> x0, local copies, waits for them, and re-layouts: 5.44 us -> none  [quarter_rows(): shaped[:, slot_index].reshape((rollouts * quarter,) + source.shape[1:])]
    reduce_sum x4 -> x0, other arithmetic: 4.92 us -> none  [the longest x2 4.11 us: shifted_sums(): return (jnp.sum(weights, axis=1), jnp.sum(weights * shifted, axis=1))]
    reduce_max x3 -> x0, other arithmetic: 3.61 us -> none  [the longest x2 2.32 us: tile_peak(): return jnp.max(logit_tile, axis=1).astype(jnp.float32)]
    dot_general x8 -> x0, matrix products: 2.85 us -> none  [table_dot(): return jnp.dot(left_side, right_side, precision=highest)]
where the time goes in v1:
time: 23.3 us; the launch traced here: 23.1 us
  Pallas kernels  22.5 us (97%)
  between operations  0.64 us (3%)
    pallas_call x1, Pallas kernels, shards(): pl.pallas_call(functools.partial(kernel, dp_size, mp_size), out_shape=(ja...  20.6 us
    pallas_call x1, Pallas kernels, shards(): pl.pallas_call(hand_over, out_shape=[jax.ShapeDtypeStruct(value.shape, va...  1.83 us

profile of v1, /device:TPU:0, one launch (start us, length us, event | category | flops | bytes accessed | tf_op | source)
XLA Modules:
  0.0 23.1 jit_solution(1714761987205639424)
XLA Ops:
  0.6 20.6 %shard_map.101 = (f32[1,8]{1,0:T(1,128)}, f32[4,128]{1,0:T(4,128)}, f32[4,128]{1,0:T(4,128)}, f32[4,128]{1,0:T(4,128)}, f32[1,1]{1,0:T(1,128)}) custom-call(s32[8]{0:T(128)} %rewards_s.1, s32[8]{0:T(128)} %groups_s.1, s32[8]{0:T(128)} %lengths_s.1, s32[1,8]{1,0:T(1,128)} %bitcast.11, s32[1,8]{1,0:T(1,128)} %bitcast.12, s32[4,128]{1,0:T(4,128)} %bitcast.9, ...), custom_call_target="tpu_custom_call" | custom-call | tf_op jit(solution)/shard_map/pallas_call | solution.py:315
  21.3 1.8 %shard_map.102 = (f32[1,8]{1,0:T(1,128)}, f32[4,128]{1,0:T(4,128)}, f32[4,128]{1,0:T(4,128)}, f32[4,128]{1,0:T(4,128)}, f32[1,1]{1,0:T(1,128)}) custom-call(f32[1,8]{1,0:T(1,128)} %get-tuple-element.15.refs_0_, f32[4,128]{1,0:T(4,128)} %get-tuple-element.16.refs_1_, f32[4,128]{1,0:T(4,128)} %get-tuple-element.17.refs_2_, ...), custom_call_target="tpu_custom_call" | custom-call | tf_op jit(solution)/shard_map/pallas_call | solution.py:355

commit v2 on v1

--- a/solution.py
+++ b/solution.py
@@ -12,6 +12,9 @@
 LANES = 128
 STEP = 16
 CHUNKS = 8
+SUM_ROWS = 16
+SUM_TILES = 64
+PARTS = 4
 
 spread_floor = 0.25
 reward_unit = 1024.0
@@ -29,6 +32,16 @@
 def kernel(
     dp_size,
     mp_size,
+    rewards_hbm,
+    groups_hbm,
+    lengths_hbm,
+    rewards_row_hbm,
+    groups_row_hbm,
+    mask_hbm,
+    targets_hbm,
+    logits_hbm,
+    result,
+    block_rows,
     rewards_s,
     groups_s,
     lengths_s,
@@ -36,53 +49,58 @@
     groups_v,
     mask_v,
     targets_v,
-    logits_hbm,
-    advantage_out,
-    weight_out,
-    logprob_out,
-    entropy_out,
-    objective_out,
-    *scratch,
+    peak_rows,
+    total_rows_ref,
+    moment_rows,
+    target_rows,
+    columns,
+    stats,
+    gathered,
+    facts,
+    facts_all,
+    part,
+    parts,
+    load_sem,
+    small_sem,
+    stat_send,
+    stat_recv,
+    fact_send,
+    fact_recv,
+    part_send,
+    part_recv,
 ):
-    chunks = scratch[:CHUNKS]
-    (
-        peak_rows,
-        total_rows_ref,
-        moment_rows,
-        target_rows,
-        columns,
-        stats,
-        gathered,
-        facts,
-        facts_all,
-        part,
-        parts,
-        load_sem,
-        stat_send,
-        stat_recv,
-        fact_send,
-        fact_recv,
-        part_send,
-        part_recv,
-    ) = scratch[CHUNKS:]
     rows, vocab = logits_hbm.shape
     rollouts = rewards_v.shape[1]
     bands = rows // LANES
     groups = rollouts * dp_size // GROUP
-    chunk_rows = rows // CHUNKS
     tiles = vocab // LANES
     me_dp = lax.axis_index("dp")
     me_mp = lax.axis_index("mp")
     f32 = jnp.float32
 
-    loads = [
-        pltpu.make_async_copy(
-            logits_hbm.at[pl.ds(c * chunk_rows, chunk_rows), :], chunks[c], load_sem.at[c]
-        )
-        for c in range(CHUNKS)
+    def load(i):
+        span = pl.ds(pl.multiple_of(i * STEP, STEP), STEP)
+        return pltpu.make_async_copy(logits_hbm.at[span, :], block_rows.at[span, :], load_sem.at[i])
+
+    steps = rows // STEP
+    for i in range(steps):
+        load(i).start()
+    small = [
+        pltpu.make_async_copy(source, target, small_sem.at[k])
+        for k, (source, target) in enumerate(
+            (
+                (rewards_hbm, rewards_s),
+                (groups_hbm, groups_s),
+                (lengths_hbm, lengths_s),
+                (rewards_row_hbm, rewards_v),
+                (groups_row_hbm, groups_v),
+                (mask_hbm, mask_v),
+                (targets_hbm, targets_v),
+            )
+        )
     ]
-    for load in loads:
-        load.start()
+    for copy in small:
+        copy.start()
 
     barrier = pltpu.get_barrier_semaphore()
 
@@ -96,6 +114,9 @@
 
     each(1, mp_size, greet_mp)
     each(1, dp_size, greet_dp)
+
+    for copy in small:
+        copy.wait()
 
     lane = lax.broadcasted_iota(jnp.int32, (bands, LANES), 1)
     band = lax.broadcasted_iota(jnp.int32, (bands, LANES), 0)
@@ -120,65 +141,82 @@
         spread_out = jnp.broadcast_to(targets_v[b : b + 1, :], (LANES, LANES))
         columns[b * LANES : (b + 1) * LANES, :] = spread_out.T
 
-    for c in range(CHUNKS):
-        loads[c].wait()
-        chunk = chunks[c]
-
-        def step(i, carry, c=c, chunk=chunk):
-            start = pl.multiple_of(i * STEP, STEP)
-            where_out = pl.ds(pl.multiple_of(c * chunk_rows + i * STEP, STEP), STEP)
-            span = pl.ds(start, STEP)
-            column = lax.shift_right_arithmetic(columns[where_out, :] - base, 7)
-            bits = [
-                jnp.bitwise_and(lax.shift_right_arithmetic(column, k), 1).astype(f32)
-                for k in range(max(tiles - 1, 0).bit_length())
-            ]
-            bits = [bit.astype(jnp.bfloat16) > 0.5 for bit in bits]
-
-            def survey(first, size):
-                if size == 1:
-                    tile = chunk[span, first * LANES : (first + 1) * LANES]
-                    return tile, tile
-                half = size // 2
-                low = survey(first, half)
-                if first + half >= tiles:
-                    return low
-                top = survey(first + half, half)
-                chosen = jnp.where(bits[half.bit_length() - 1], top[1], low[1])
-                return jnp.maximum(low[0], top[0]), chosen
-
-            high, held = survey(0, 1 << max(tiles - 1, 0).bit_length())
-            target_rows[where_out, :] = held.astype(f32)
-            high = high.astype(f32)
-            total = jnp.zeros((STEP, LANES), f32)
-            moment = jnp.zeros((STEP, LANES), f32)
-            for j in range(tiles):
-                shifted = chunk[span, j * LANES : (j + 1) * LANES].astype(f32) - high
+    levels = max(tiles - 1, 0).bit_length()
+
+    def survey_step(i, carry):
+        load(i).wait()
+        span = pl.ds(pl.multiple_of(i * STEP, STEP), STEP)
+        column = lax.shift_right_arithmetic(columns[span, :] - base, 7)
+        bits = [
+            jnp.bitwise_and(lax.shift_right_arithmetic(column, k), 1).astype(f32)
+            for k in range(levels)
+        ]
+        bits = [bit.astype(jnp.bfloat16) > 0.5 for bit in bits]
+
+        def survey(first, size):
+            if size == 1:
+                tile = block_rows[span, first * LANES : (first + 1) * LANES]
+                return tile, tile
+            half = size // 2
+            low = survey(first, half)
+            if first + half >= tiles:
+                return low
+            top = survey(first + half, half)
+            chosen = jnp.where(bits[half.bit_length() - 1], top[1], low[1])
+            return jnp.maximum(low[0], top[0]), chosen
+
+        high, held = survey(0, 1 << levels)
+        target_rows[span, :] = held.astype(f32)
+        peak_rows[span, :] = high.astype(f32)
+        return carry
+
+    block = min(SUM_TILES, tiles)
+
+    def sum_step(i, carry):
+        span = pl.ds(pl.multiple_of(i * SUM_ROWS, SUM_ROWS), SUM_ROWS)
+        high = peak_rows[span, :]
+
+        def add_block(q, sums):
+            totals, moments = list(sums[:PARTS]), list(sums[PARTS:])
+            for j in range(block):
+                at = pl.ds(pl.multiple_of((q * block + j) * LANES, LANES), LANES)
+                shifted = block_rows[span, at].astype(f32) - high
                 weight = jnp.exp(shifted)
-                total += weight
-                moment += weight * shifted
-            peak_rows[where_out, :] = high
-            total_rows_ref[where_out, :] = total
-            moment_rows[where_out, :] = moment
-            return carry
-
-        lax.fori_loop(0, chunk_rows // STEP, step, 0)
-
-        if c == 0:
-            pl.semaphore_wait(barrier, mp_size + dp_size - 2)
-
-            def send_fact(k):
-                peer = lax.rem(me_dp + k, dp_size)
-                pltpu.make_async_remote_copy(
-                    src_ref=facts,
-                    dst_ref=facts_all.at[me_dp],
-                    send_sem=fact_send.at[k],
-                    recv_sem=fact_recv.at[me_dp],
-                    device_id=(peer, me_mp),
-                    device_id_type=MESH,
-                ).start()
-
-            each(1, dp_size, send_fact)
+                totals[j % PARTS] += weight
+                moments[j % PARTS] += weight * shifted
+            return (*totals, *moments)
+
+        zero = jnp.zeros((SUM_ROWS, LANES), f32)
+        sums = lax.fori_loop(0, tiles // block, add_block, (zero,) * (2 * PARTS))
+        total_rows_ref[span, :] = functools.reduce(jnp.add, sums[:PARTS])
+        moment_rows[span, :] = functools.reduce(jnp.add, sums[PARTS:])
+        return carry
+
+    def chunk_step(c, carry):
+        first = c * (steps // CHUNKS)
+        lax.fori_loop(first, first + steps // CHUNKS, survey_step, 0)
+        low = c * (rows // SUM_ROWS // CHUNKS)
+        lax.fori_loop(low, low + rows // SUM_ROWS // CHUNKS, sum_step, 0)
+        return carry
+
+    split = CHUNKS - 2
+    lax.fori_loop(0, split, chunk_step, 0)
+    pl.semaphore_wait(barrier, mp_size + dp_size - 2)
+
+    def fact_copy(k, slot):
+        peer = lax.rem(me_dp + k, dp_size)
+        return pltpu.make_async_remote_copy(
+            src_ref=facts,
+            dst_ref=facts_all.at[slot],
+            send_sem=fact_send.at[k],
+            recv_sem=fact_recv.at[slot],
+            device_id=(peer, me_mp),
+            device_id_type=MESH,
+        )
+
+    each(1, dp_size, lambda k: fact_copy(k, me_dp).start())
+    facts_all[me_dp] = facts[...]
+    lax.fori_loop(split, CHUNKS, chunk_step, 0)
 
     sub = lax.broadcasted_iota(jnp.int32, (LANES, LANES), 0)
     for b in range(bands):
@@ -216,18 +254,6 @@
     each(1, mp_size, lambda k: stat_copy(k, me_mp).start())
     gathered[me_mp] = stats[...]
 
-    def fact_copy(k, slot):
-        peer = lax.rem(me_dp + k, dp_size)
-        return pltpu.make_async_remote_copy(
-            src_ref=facts,
-            dst_ref=facts_all.at[slot],
-            send_sem=fact_send.at[k],
-            recv_sem=fact_recv.at[slot],
-            device_id=(peer, me_mp),
-            device_id_type=MESH,
-        )
-
-    facts_all[me_dp] = facts[...]
     each(1, dp_size, lambda k: fact_copy(k, lax.rem(me_dp + dp_size - k, dp_size)).wait_recv())
     all_reward = facts_all[:, 0:bands, :]
     all_group = facts_all[:, bands : 2 * bands, :]
@@ -257,9 +283,9 @@
         mean_tok = jnp.where(in_tok, mean, mean_tok)
         spread_tok = jnp.where(in_tok, spread, spread_tok)
         scale_tok = jnp.where(in_tok, scale, scale_tok)
-    advantage_out[...] = (reward_row - mean_row) / spread_row
+    result[3 * bands : 3 * bands + 1, 0:rollouts] = (reward_row - mean_row) / spread_row
     weight = live * ((reward_tok - mean_tok) / spread_tok * scale_tok)
-    weight_out[...] = weight
+    result[0:bands, :] = weight
 
     each(1, mp_size, lambda k: stat_copy(k, lax.rem(me_mp + mp_size - k, mp_size)).wait_recv())
     peaks = gathered[:, 0:bands, :]
@@ -272,7 +298,7 @@
     target = jnp.sum(gathered[:, 3 * bands : 4 * bands, :], axis=0)
     log_total = jnp.log(total)
     logprob = live * (target - (peak + log_total))
-    logprob_out[...] = logprob
+    result[bands : 2 * bands, :] = logprob
     own = jnp.sum(jnp.sum(weight * logprob, axis=1, keepdims=True), axis=0, keepdims=True)
     part[...] = jnp.broadcast_to(own, part.shape)
 
@@ -289,20 +315,23 @@
 
     each(1, dp_size, lambda k: part_copy(k, me_dp).start())
     parts[me_dp] = part[...]
-    entropy_out[...] = live * (log_total - moment / total)
+    result[2 * bands : 3 * bands, :] = live * (log_total - moment / total)
 
     each(1, dp_size, lambda k: fact_copy(k, me_dp).wait_send())
     each(1, mp_size, lambda k: stat_copy(k, me_mp).wait_send())
     each(1, dp_size, lambda k: part_copy(k, lax.rem(me_dp + dp_size - k, dp_size)).wait_recv())
     summed = jnp.sum(parts[...], axis=0)[0:1, 0:1]
-    objective_out[...] = -summed / (groups * GROUP * WIN)
+    result[3 * bands + 1 : 3 * bands + 2, 0:1] = -summed / (groups * GROUP * WIN)
     each(1, dp_size, lambda k: part_copy(k, me_dp).wait_send())
 
 
-def hand_over(*refs):
-    half = len(refs) // 2
-    for source, result in zip(refs[:half], refs[half:]):
-        result[...] = source[...]
+def hand_over(result, advantage, weight, logprob, entropy, objective):
+    bands = weight.shape[0]
+    weight[...] = result[0:bands, :]
+    logprob[...] = result[bands : 2 * bands, :]
+    entropy[...] = result[2 * bands : 3 * bands, :]
+    advantage[...] = result[3 * bands : 3 * bands + 1, 0 : advantage.shape[1]]
+    objective[...] = result[3 * bands + 1 : 3 * bands + 2, 0:1]
 
 
 def shards(dp_size, mp_size, rewards, group_ids, lengths, token_mask, targets, logits):
@@ -310,20 +339,17 @@
     rollouts = lengths.shape[0]
     bands = rows // LANES
     f32 = jnp.float32
-    smem = pl.BlockSpec(memory_space=pltpu.SMEM)
+    anywhere = pl.BlockSpec(memory_space=pl.ANY)
     vmem = pl.BlockSpec(memory_space=pltpu.VMEM)
-    outs = pl.pallas_call(
+    result = pl.pallas_call(
         functools.partial(kernel, dp_size, mp_size),
-        out_shape=(
-            jax.ShapeDtypeStruct((1, rollouts), f32),
-            jax.ShapeDtypeStruct((bands, LANES), f32),
-            jax.ShapeDtypeStruct((bands, LANES), f32),
-            jax.ShapeDtypeStruct((bands, LANES), f32),
-            jax.ShapeDtypeStruct((1, 1), f32),
-        ),
-        in_specs=[smem] * 3 + [vmem] * 4 + [pl.BlockSpec(memory_space=pl.ANY)],
-        out_specs=(vmem,) * 5,
-        scratch_shapes=[pltpu.VMEM((rows // CHUNKS, vocab), logits.dtype)] * CHUNKS
+        out_shape=jax.ShapeDtypeStruct((3 * bands + 2, LANES), f32),
+        in_specs=[anywhere] * 8,
+        out_specs=vmem,
+        scratch_shapes=[pltpu.VMEM((rows, vocab), logits.dtype)]
+        + [pltpu.SMEM((rollouts,), jnp.int32)] * 3
+        + [pltpu.VMEM((1, rollouts), jnp.int32)] * 2
+        + [pltpu.VMEM((bands, LANES), jnp.int32)] * 2
         + [pltpu.VMEM((rows, LANES), f32)] * 4
         + [pltpu.VMEM((rows, LANES), jnp.int32)]
         + [
@@ -333,7 +359,8 @@
             pltpu.VMEM((dp_size, 3 * bands, LANES), f32),
             pltpu.VMEM((8, LANES), f32),
             pltpu.VMEM((dp_size, 8, LANES), f32),
-            pltpu.SemaphoreType.DMA((CHUNKS,)),
+            pltpu.SemaphoreType.DMA((rows // STEP,)),
+            pltpu.SemaphoreType.DMA((7,)),
             pltpu.SemaphoreType.DMA((mp_size,)),
             pltpu.SemaphoreType.DMA((mp_size,)),
             pltpu.SemaphoreType.DMA((dp_size,)),
@@ -352,13 +379,18 @@
         targets.reshape(bands, LANES),
         logits,
     )
-    outs = pl.pallas_call(
+    advantage, weight, logprob, entropy, objective = pl.pallas_call(
         hand_over,
-        out_shape=[jax.ShapeDtypeStruct(value.shape, value.dtype) for value in outs],
-        in_specs=[vmem] * 5,
+        out_shape=(
+            jax.ShapeDtypeStruct((1, rollouts), f32),
+            jax.ShapeDtypeStruct((bands, LANES), f32),
+            jax.ShapeDtypeStruct((bands, LANES), f32),
+            jax.ShapeDtypeStruct((bands, LANES), f32),
+            jax.ShapeDtypeStruct((1, 1), f32),
+        ),
+        in_specs=[vmem],
         out_specs=[vmem] * 5,
-    )(*outs)
-    advantage, weight, logprob, entropy, objective = outs
+    )(result)
     return (
         advantage.reshape(-1),
         weight.reshape(-1),

time: 23.3 us -> 23.7 us (1.017)
  Pallas kernels: 22.5 us -> 22.9 us
    pallas_call x2, Pallas kernels: 22.5 us -> 22.9 us  [the longest x1 21.6 us: shards(): pl.pallas_call(functools.partial(kernel, dp_size, mp_size), out_shape=jax...]
where the time goes in v2:
time: 23.7 us; the launch traced here: 23.5 us
  Pallas kernels  22.9 us (97%)
  between operations  0.64 us (3%)
    pallas_call x1, Pallas kernels, shards(): pl.pallas_call(functools.partial(kernel, dp_size, mp_size), out_shape=jax...  21.6 us
    pallas_call x1, Pallas kernels, shards(): pl.pallas_call(hand_over, out_shape=(jax.ShapeDtypeStruct((1, rollouts),...  1.29 us

profile of v2, /device:TPU:0, one launch (start us, length us, event | category | flops | bytes accessed | tf_op | source)
XLA Modules:
  0.0 23.5 jit_solution(2936639275294779794)
XLA Ops:
  0.6 21.6 %shard_map.101.result = f32[14,128]{1,0:T(8,128)} custom-call(s32[8]{0:T(128)} %rewards_hbm.1, s32[8]{0:T(128)} %groups_hbm.1, s32[8]{0:T(128)} %lengths_hbm.1, s32[1,8]{1,0:T(1,128)} %bitcast.11, s32[1,8]{1,0:T(1,128)} %bitcast.12, s32[4,128]{1,0:T(4,128)} %bitcast.9, s32[4,128]{1,0:T(4,128)} %bitcast.10, bf16[512,8192]{1,0:T(8,128)(2,1)} %logits_hbm.1), custom_call_target="tpu_custom_call" | custom-call | tf_op jit(solution)/shard_map/pallas_call | solution.py:344
  22.2 1.3 %shard_map.102 = (f32[1,8]{1,0:T(1,128)}, f32[4,128]{1,0:T(4,128)}, f32[4,128]{1,0:T(4,128)}, f32[4,128]{1,0:T(4,128)}, f32[1,1]{1,0:T(1,128)}) custom-call(f32[14,128]{1,0:T(8,128)} %shard_map.101.result), custom_call_target="tpu_custom_call" | custom-call | tf_op jit(solution)/shard_map/pallas_call | solution.py:382

commit v3 on v2

--- a/solution.py
+++ b/solution.py
@@ -15,6 +15,7 @@
 SUM_ROWS = 16
 SUM_TILES = 64
 PARTS = 4
+AHEAD = 8
 
 spread_floor = 0.25
 reward_unit = 1024.0
@@ -83,7 +84,7 @@
         return pltpu.make_async_copy(logits_hbm.at[span, :], block_rows.at[span, :], load_sem.at[i])
 
     steps = rows // STEP
-    for i in range(steps):
+    for i in range(min(AHEAD, steps)):
         load(i).start()
     small = [
         pltpu.make_async_copy(source, target, small_sem.at[k])
@@ -145,6 +146,11 @@
 
     def survey_step(i, carry):
         load(i).wait()
+
+        @pl.when(i + AHEAD < steps)
+        def _():
+            load(i + AHEAD).start()
+
         span = pl.ds(pl.multiple_of(i * STEP, STEP), STEP)
         column = lax.shift_right_arithmetic(columns[span, :] - base, 7)
         bits = [
@@ -199,7 +205,7 @@
         lax.fori_loop(low, low + rows // SUM_ROWS // CHUNKS, sum_step, 0)
         return carry
 
-    split = CHUNKS - 2
+    split = CHUNKS // 2
     lax.fori_loop(0, split, chunk_step, 0)
     pl.semaphore_wait(barrier, mp_size + dp_size - 2)
 

time: 23.7 us -> 22 us (0.928)
  Pallas kernels: 22.9 us -> 21.1 us
    pallas_call x1, Pallas kernels: 21.6 us -> 19.8 us  [shards(): pl.pallas_call(functools.partial(kernel, dp_size, mp_size), out_shape=jax...]
where the time goes in v3:
time: 22 us; the launch traced here: 21.8 us
  Pallas kernels  21.1 us (96%)
  between operations  0.64 us (3%)
    pallas_call x1, Pallas kernels, shards(): pl.pallas_call(functools.partial(kernel, dp_size, mp_size), out_shape=jax...  19.8 us
    pallas_call x1, Pallas kernels, shards(): pl.pallas_call(hand_over, out_shape=(jax.ShapeDtypeStruct((1, rollouts),...  1.29 us

profile of v3, /device:TPU:0, one launch (start us, length us, event | category | flops | bytes accessed | tf_op | source)
XLA Modules:
  0.0 21.8 jit_solution(5123085949481183679)
XLA Ops:
  0.6 19.8 %shard_map.101.result = f32[14,128]{1,0:T(8,128)} custom-call(s32[8]{0:T(128)} %rewards_hbm.1, s32[8]{0:T(128)} %groups_hbm.1, s32[8]{0:T(128)} %lengths_hbm.1, s32[1,8]{1,0:T(1,128)} %bitcast.11, s32[1,8]{1,0:T(1,128)} %bitcast.12, s32[4,128]{1,0:T(4,128)} %bitcast.9, s32[4,128]{1,0:T(4,128)} %bitcast.10, bf16[512,8192]{1,0:T(8,128)(2,1)} %logits_hbm.1), custom_call_target="tpu_custom_call" | custom-call | tf_op jit(solution)/shard_map/pallas_call | solution.py:350
  20.5 1.3 %shard_map.102 = (f32[1,8]{1,0:T(1,128)}, f32[4,128]{1,0:T(4,128)}, f32[4,128]{1,0:T(4,128)}, f32[4,128]{1,0:T(4,128)}, f32[1,1]{1,0:T(1,128)}) custom-call(f32[14,128]{1,0:T(8,128)} %shard_map.101.result), custom_call_target="tpu_custom_call" | custom-call | tf_op jit(solution)/shard_map/pallas_call | solution.py:388
